TPU v7x, 32 devices: a whole 2x2x4 slice. The times are simulated.
32 devices in a mesh: groups: 2 (over y), graph: 16 (over z, x, core).
Axes of the slice: x: 2, y: 2, z: 4, core: 2. Of those that a mesh axis runs over, the one named last changes fastest.
Arguments:
- edge_state: bfloat16 [8192, 512], P(('groups', 'graph')), parts along dimension 0, may hold values from -6 to 6
- atom_state: bfloat16 [512, 256], P(('groups', 'graph')), parts along dimension 0, may hold values from -6 to 6
- atom_sends: int32 [4096], P(('groups', 'graph')), parts along dimension 0, may hold values from 0 to 15
- edge_source: int32 [8192], P(('groups', 'graph')), parts along dimension 0, may hold values from 0 to 127
- edge_target: int32 [8192], P(('groups', 'graph')), parts along dimension 0, may hold values from 0 to 15
- send_edges: int32 [262144], P(('groups', 'graph')), parts along dimension 0, may hold values from 0 to 255
- triplet_in: int32 [262144], P(('groups', 'graph')), parts along dimension 0, may hold values from 0 to 8191, as said below
- triplet_out: int32 [262144], P(('groups', 'graph')), parts along dimension 0, may hold values from 0 to 8191, as said below
- triplet_valid: int32 [262144], P(('groups', 'graph')), parts along dimension 0, may hold values 0 or 1
- triplet_basis: bfloat16 [16, 262144], P(None, ('groups', 'graph')), parts along dimension 1, may hold values from -6 to 6
- return_edges: int32 [262144], P(('groups', 'graph')), parts along dimension 0, may hold values from 0 to 255
- w_edge: bfloat16 [512, 512], replicated, may hold values from -0.25 to 0.25
- w_source: bfloat16 [256, 512], replicated, may hold values from -0.375 to 0.375
- w_down: bfloat16 [512, 64], replicated, may hold values from -0.25 to 0.25
- w_bilinear: bfloat16 [64, 1024], replicated, may hold values from -0.1875 to 0.1875
- w_up: bfloat16 [64, 512], replicated, may hold values from -0.125 to 0.125
- w_residual: bfloat16 [4, 512, 512], replicated, may hold values from -0.25 to 0.25
- w_atom: bfloat16 [512, 256], replicated, may hold values from -0.25 to 0.25
Outputs:
- edge_out: bfloat16 [8192, 512], P(('groups', 'graph')), parts along dimension 0
- atom_out: bfloat16 [512, 256], P(('groups', 'graph')), parts along dimension 0
There are 2 independent parts, one for each index of `groups`. A program takes and returns all parts, laid end to end along the dimension named above; an argument that names none is the same for every part. Nothing has to cross between parts.
Inputs may be any that keep to these rules, and one draw needn't show every extreme that they name: `atom_sends`: entry d * 8 + c of a device's 128 entries is sent to device d. `send_edges`: entry t * 512 + c of a device's 8192 entries is sent to tile t. `triplet_in`: triplet j of a tile reads a received slot in the same aligned block of 512 slots as j. `triplet_out`: slot d * 512 + c of a tile is returned to device d; triplet j of a tile adds to a slot in the same aligned block of 512 slots as j. `return_edges`: entry t * 512 + c of a device's 8192 entries belongs to the slot that tile t returns in place c.
All inputs are finite; a program needn't handle non-finite values. No bound on the sum of `triplet_valid` on one device may be relied on, other than what follows from the above.
Results may differ from a plain program's by a relative error of at most 0.0095.
Values may be sent and summed in bfloat16 or wider, within the bound.
A program may use at most 64 MiB of HBM per device.

v0:
```python
import jax
import jax.numpy as jnp
from jax import lax
from jax.sharding import PartitionSpec as P

WIN = 512


inv_root = 0.7071067811865476


def matmul(left, right):
    return jnp.dot(left, right, preferred_element_type=jnp.float32)


def pick_rows(indices, table):
    chooser = (indices[:, None] == jnp.arange(table.shape[0], dtype=jnp.int32)[None, :]).astype(
        table.dtype
    )
    return matmul(chooser, table).astype(table.dtype)


def bilinear_terms(inputs_x, coeffs, keeps, w_bilinear):
    expanded = matmul(inputs_x, w_bilinear)
    expanded = expanded.reshape(inputs_x.shape[0], coeffs.shape[0], -1)
    mixed = jnp.einsum("tkd,kt->td", expanded, coeffs.astype(jnp.float32))
    return mixed * keeps.astype(jnp.float32)[:, None]


def tile_sums(slot_rows, local_in, local_out, keeps, coeffs, w_bilinear):
    trip_count = slot_rows.shape[0]
    block_size = WIN
    block_count = trip_count // block_size
    basis_rows = coeffs.shape[0]
    block_iota = jnp.arange(block_size, dtype=jnp.int32)

    def one_block(operands):
        rows_blk, in_blk, out_blk, keep_blk, coef_blk = operands
        in_hot = ((in_blk % block_size)[:, None] == block_iota[None, :]).astype(jnp.bfloat16)
        inputs_x = matmul(in_hot, rows_blk).astype(jnp.bfloat16)
        mixed = bilinear_terms(inputs_x, coef_blk, keep_blk, w_bilinear)
        out_hot = (block_iota[:, None] == (out_blk % block_size)[None, :]).astype(jnp.float32)
        return jnp.dot(
            out_hot, mixed, precision=lax.Precision.HIGHEST, preferred_element_type=jnp.float32
        )

    shaped_coeffs = jnp.transpose(coeffs.reshape(basis_rows, block_count, block_size), (1, 0, 2))
    summed = lax.map(
        one_block,
        (
            slot_rows.reshape(block_count, block_size, -1),
            local_in.reshape(block_count, block_size),
            local_out.reshape(block_count, block_size),
            keeps.reshape(block_count, block_size),
            shaped_coeffs,
        ),
    )
    return summed.reshape(trip_count, -1).astype(jnp.bfloat16)


def on_device(
    edge_state,
    atom_state,
    atom_sends,
    edge_source,
    edge_target,
    send_edges,
    triplet_in,
    triplet_out,
    triplet_valid,
    triplet_basis,
    return_edges,
    w_edge,
    w_source,
    w_down,
    w_bilinear,
    w_up,
    w_residual,
    w_atom,
):
    edge_count = edge_state.shape[0]
    atom_count = atom_state.shape[0]
    arrived_atoms = lax.all_to_all(
        pick_rows(atom_sends, atom_state), "graph", split_axis=0, concat_axis=0, tiled=True
    )
    src_rows = pick_rows(edge_source, arrived_atoms)
    pre_act = matmul(edge_state, w_edge) + matmul(src_rows, w_source)
    activated = jax.nn.silu(pre_act).astype(jnp.bfloat16)
    projected = jax.nn.silu(matmul(activated, w_down)).astype(jnp.bfloat16)
    slot_rows = lax.all_to_all(
        pick_rows(send_edges, projected), "graph", split_axis=0, concat_axis=0, tiled=True
    )
    slot_sums = tile_sums(
        slot_rows, triplet_in, triplet_out, triplet_valid, triplet_basis, w_bilinear
    )
    returned = lax.all_to_all(slot_sums, "graph", split_axis=0, concat_axis=0, tiled=True)
    back_hot = (jnp.arange(edge_count, dtype=jnp.int32)[:, None] == return_edges[None, :]).astype(
        jnp.bfloat16
    )
    aggregate = matmul(back_hot, returned)
    update = jax.nn.silu(matmul(aggregate.astype(jnp.bfloat16), w_up))
    base = ((edge_state.astype(jnp.float32) + activated.astype(jnp.float32)) * inv_root).astype(
        jnp.bfloat16
    )
    inner_one = jax.nn.silu(matmul(base, w_residual[0])).astype(jnp.bfloat16)
    middle = (
        (base.astype(jnp.float32) + jax.nn.silu(matmul(inner_one, w_residual[1]))) * inv_root
    ).astype(jnp.bfloat16)
    inner_two = jax.nn.silu(matmul(middle, w_residual[2])).astype(jnp.bfloat16)
    chain = (middle.astype(jnp.float32) + jax.nn.silu(matmul(inner_two, w_residual[3]))) * inv_root
    edge_out = (chain + update).astype(jnp.bfloat16)
    contrib = matmul(edge_out, w_atom).astype(jnp.bfloat16)
    one_hot = (edge_target[None, :] == jnp.arange(atom_count, dtype=jnp.int32)[:, None]).astype(
        jnp.bfloat16
    )
    atom_sum = matmul(one_hot, contrib)
    atom_out = (atom_state.astype(jnp.float32) + jax.nn.silu(0.25 * atom_sum)).astype(jnp.bfloat16)
    return (edge_out, atom_out)


def solution(mesh):
    placed = (
        P(("groups", "graph"), None),
        P(("groups", "graph"), None),
        P(("groups", "graph")),
        P(("groups", "graph")),
        P(("groups", "graph")),
        P(("groups", "graph")),
        P(("groups", "graph")),
        P(("groups", "graph")),
        P(("groups", "graph")),
        P(None, ("groups", "graph")),
        P(("groups", "graph")),
        P(),
        P(),
        P(),
        P(),
        P(),
        P(),
        P(),
    )
    return jax.shard_map(
        on_device,
        mesh=mesh,
        in_specs=placed,
        out_specs=(P(("groups", "graph"), None), P(("groups", "graph"), None)),
        check_vma=False,
    )
```

profile of v0, /device:TPU:0, one launch (start us, length us, event | category | flops | bytes accessed | tf_op | source)
XLA Modules:
  0.0 138.6 jit_solution(2237447407892621800)
XLA Ops:
  0.6 1.6 %fusion.21 = bf16[16,8,256]{2,1,0:T(8,128)(2,1)} fusion(bf16[16,256]{1,0:T(8,128)(2,1)} %param.21, s32[128]{0:T(128)} %param.22), kind=kOutput, calls=%fused_computation.37 | convolution fusion | flops 1083392 | bytes 74240 | tf_op jit(solution)/shard_map/dot_general | solution.py:13
  2.3 7.5 %all-to-all-start = ((bf16[16,8,256]{2,1,0:T(8,128)(2,1)}), bf16[16,8,256]{2,1,0:T(8,128)(2,1)S(1)}, u32[]{:S(2)}, u32[]{:S(2)}) async-start(bf16[16,8,256]{2,1,0:T(8,128)(2,1)} %fusion.21), calls=%async_computation | async-start | bytes 131072 | tf_op jit(solution)/shard_map/all_to_all | solution.py:83
  9.8 1.2 fusion.67
  11.0 5.6 %all-to-all-done = bf16[16,8,256]{2,1,0:T(8,128)(2,1)S(1)} async-done(((bf16[16,8,256]{2,1,0:T(8,128)(2,1)}), bf16[16,8,256]{2,1,0:T(8,128)(2,1)S(1)}, u32[]{:S(2)}, u32[]{:S(2)}) %all-to-all-start) | async-done | bytes 65568 | tf_op jit(solution)/shard_map/all_to_all | solution.py:83
  16.7 1.4 %multiply_convert_fusion.4 = bf16[256,512]{1,0:T(8,128)(2,1)S(1)} fusion(f32[256,512]{1,0:T(8,128)S(1)} %fusion.67, bf16[256,512]{1,0:T(8,128)(2,1)} %param.32, bf16[16,8,256]{2,1,0:T(8,128)(2,1)S(1)} %all-to-all-done, s32[256]{0:T(256)} %param.23), kind=kOutput, calls=%fused_computation.59 | convolution fusion | flops 84770816 | bytes 1115136 | tf_op jit(solution)/shard_map/dot_general | solution.py:13
  18.1 1.9 %convolution_convert_fusion.1 = bf16[8192,64]{0,1:T(8,128)(2,1)S(1)} fusion(s32[8192]{0:T(1024)S(1)} %copy-done.11, bf16[256,512]{1,0:T(8,128)(2,1)S(1)} %multiply_convert_fusion.4, bf16[512,64]{0,1:T(8,128)(2,1)S(1)} %copy-done.9), kind=kOutput, calls=%fused_computation.26 | convolution fusion | flops 287916032 | bytes 1409024 | tf_op jit(solution)/shard_map/dot_general | solution.py:13
  20.1 1.1 copy.44
  21.2 4.5 %all-to-all-start.1 = ((bf16[16,512,64]{1,2,0:T(8,128)(2,1)}), bf16[16,512,64]{1,2,0:T(8,128)(2,1)}, u32[]{:S(2)}, u32[]{:S(2)}) async-start(bf16[16,512,64]{1,2,0:T(8,128)(2,1)} %bitcast.66), calls=%async_computation.1 | async-start | bytes 2097152 | tf_op jit(solution)/shard_map/all_to_all | solution.py:90
  26.0 22.6 %all-to-all-done.1 = bf16[16,512,64]{1,2,0:T(8,128)(2,1)} async-done(((bf16[16,512,64]{1,2,0:T(8,128)(2,1)}), bf16[16,512,64]{1,2,0:T(8,128)(2,1)}, u32[]{:S(2)}, u32[]{:S(2)}) %all-to-all-start.1) | async-done | bytes 1048608 | tf_op jit(solution)/shard_map/all_to_all | solution.py:90
  48.6 56.3 %while.14 = (s32[]{:T(128)}, bf16[16,512,64]{1,2,0:T(8,128)(2,1)}, s32[16,512]{1,0:T(8,128)S(1)}, s32[16,512]{1,0:T(8,128)S(1)}, bf16[16,512,64]{1,2,0:T(8,128)(...) while((s32[]{:T(128)}, bf16[16,512,64]{1,2,0:T(8,128)(2,1)}, ...), condition=%wide.region_1.2_spmd.clone.clone, body=%wide.region_0.1_spmd.clone.clone.sunk | while | flops 303615488 | bytes 5150841 | solution.py:48
  48.6 1.7 %fusion.88 = f32[512,1024]{0,1:T(8,128)S(1)} fusion(bf16[64,1024]{1,0:T(8,128)(2,1)S(1)} %get-tuple-element.270, s32[512]{0:T(512)S(1)} %add_select_fusion.2, bf16[16,512,64]{1,2,0:T(8,128)(2,1)} %get-tuple-element.269, s32[]{:T(128)S(6)} %copy.50), kind=kOutput, calls=%fused_computation.5.clone.1 | convolution fusion | flops 100958208 | bytes 2295812 | tf_op jit(solution)/shard_map/while/body/eval_jaxpr/dot_general | solution.py:13
  50.3 0.3 multiply_reduce_fusion.2
  50.7 1.4 fusion.89
  52.1 1.7 %fusion.88 = f32[512,1024]{0,1:T(8,128)S(1)} fusion(bf16[64,1024]{1,0:T(8,128)(2,1)S(1)} %get-tuple-element.270, s32[512]{0:T(512)S(1)} %add_select_fusion.2, bf16[16,512,64]{1,2,0:T(8,128)(2,1)} %get-tuple-element.269, s32[]{:T(128)S(6)} %copy.50), kind=kOutput, calls=%fused_computation.5.clone.1 | convolution fusion | flops 100958208 | bytes 2295812 | tf_op jit(solution)/shard_map/while/body/eval_jaxpr/dot_general | solution.py:13
  53.8 0.3 multiply_reduce_fusion.2
  54.2 1.4 fusion.89
  55.7 1.7 %fusion.88 = f32[512,1024]{0,1:T(8,128)S(1)} fusion(bf16[64,1024]{1,0:T(8,128)(2,1)S(1)} %get-tuple-element.270, s32[512]{0:T(512)S(1)} %add_select_fusion.2, bf16[16,512,64]{1,2,0:T(8,128)(2,1)} %get-tuple-element.269, s32[]{:T(128)S(6)} %copy.50), kind=kOutput, calls=%fused_computation.5.clone.1 | convolution fusion | flops 100958208 | bytes 2295812 | tf_op jit(solution)/shard_map/while/body/eval_jaxpr/dot_general | solution.py:13
  57.4 0.3 multiply_reduce_fusion.2
  57.7 1.4 fusion.89
  59.2 1.7 %fusion.88 = f32[512,1024]{0,1:T(8,128)S(1)} fusion(bf16[64,1024]{1,0:T(8,128)(2,1)S(1)} %get-tuple-element.270, s32[512]{0:T(512)S(1)} %add_select_fusion.2, bf16[16,512,64]{1,2,0:T(8,128)(2,1)} %get-tuple-element.269, s32[]{:T(128)S(6)} %copy.50), kind=kOutput, calls=%fused_computation.5.clone.1 | convolution fusion | flops 100958208 | bytes 2295812 | tf_op jit(solution)/shard_map/while/body/eval_jaxpr/dot_general | solution.py:13
  60.9 0.3 multiply_reduce_fusion.2
  61.3 1.4 fusion.89
  62.7 1.7 %fusion.88 = f32[512,1024]{0,1:T(8,128)S(1)} fusion(bf16[64,1024]{1,0:T(8,128)(2,1)S(1)} %get-tuple-element.270, s32[512]{0:T(512)S(1)} %add_select_fusion.2, bf16[16,512,64]{1,2,0:T(8,128)(2,1)} %get-tuple-element.269, s32[]{:T(128)S(6)} %copy.50), kind=kOutput, calls=%fused_computation.5.clone.1 | convolution fusion | flops 100958208 | bytes 2295812 | tf_op jit(solution)/shard_map/while/body/eval_jaxpr/dot_general | solution.py:13
  64.4 0.3 multiply_reduce_fusion.2
  64.8 1.4 fusion.89
  66.2 1.7 %fusion.88 = f32[512,1024]{0,1:T(8,128)S(1)} fusion(bf16[64,1024]{1,0:T(8,128)(2,1)S(1)} %get-tuple-element.270, s32[512]{0:T(512)S(1)} %add_select_fusion.2, bf16[16,512,64]{1,2,0:T(8,128)(2,1)} %get-tuple-element.269, s32[]{:T(128)S(6)} %copy.50), kind=kOutput, calls=%fused_computation.5.clone.1 | convolution fusion | flops 100958208 | bytes 2295812 | tf_op jit(solution)/shard_map/while/body/eval_jaxpr/dot_general | solution.py:13
  67.9 0.3 multiply_reduce_fusion.2
  68.3 1.4 fusion.89
  69.7 1.7 %fusion.88 = f32[512,1024]{0,1:T(8,128)S(1)} fusion(bf16[64,1024]{1,0:T(8,128)(2,1)S(1)} %get-tuple-element.270, s32[512]{0:T(512)S(1)} %add_select_fusion.2, bf16[16,512,64]{1,2,0:T(8,128)(2,1)} %get-tuple-element.269, s32[]{:T(128)S(6)} %copy.50), kind=kOutput, calls=%fused_computation.5.clone.1 | convolution fusion | flops 100958208 | bytes 2295812 | tf_op jit(solution)/shard_map/while/body/eval_jaxpr/dot_general | solution.py:13
  71.4 0.3 multiply_reduce_fusion.2
  71.8 1.4 fusion.89
  73.3 1.7 %fusion.88 = f32[512,1024]{0,1:T(8,128)S(1)} fusion(bf16[64,1024]{1,0:T(8,128)(2,1)S(1)} %get-tuple-element.270, s32[512]{0:T(512)S(1)} %add_select_fusion.2, bf16[16,512,64]{1,2,0:T(8,128)(2,1)} %get-tuple-element.269, s32[]{:T(128)S(6)} %copy.50), kind=kOutput, calls=%fused_computation.5.clone.1 | convolution fusion | flops 100958208 | bytes 2295812 | tf_op jit(solution)/shard_map/while/body/eval_jaxpr/dot_general | solution.py:13
  74.9 0.3 multiply_reduce_fusion.2
  75.3 1.4 fusion.89
  76.8 1.7 %fusion.88 = f32[512,1024]{0,1:T(8,128)S(1)} fusion(bf16[64,1024]{1,0:T(8,128)(2,1)S(1)} %get-tuple-element.270, s32[512]{0:T(512)S(1)} %add_select_fusion.2, bf16[16,512,64]{1,2,0:T(8,128)(2,1)} %get-tuple-element.269, s32[]{:T(128)S(6)} %copy.50), kind=kOutput, calls=%fused_computation.5.clone.1 | convolution fusion | flops 100958208 | bytes 2295812 | tf_op jit(solution)/shard_map/while/body/eval_jaxpr/dot_general | solution.py:13
  78.5 0.3 multiply_reduce_fusion.2
  78.9 1.4 fusion.89
  80.3 1.7 %fusion.88 = f32[512,1024]{0,1:T(8,128)S(1)} fusion(bf16[64,1024]{1,0:T(8,128)(2,1)S(1)} %get-tuple-element.270, s32[512]{0:T(512)S(1)} %add_select_fusion.2, bf16[16,512,64]{1,2,0:T(8,128)(2,1)} %get-tuple-element.269, s32[]{:T(128)S(6)} %copy.50), kind=kOutput, calls=%fused_computation.5.clone.1 | convolution fusion | flops 100958208 | bytes 2295812 | tf_op jit(solution)/shard_map/while/body/eval_jaxpr/dot_general | solution.py:13
  82.0 0.3 multiply_reduce_fusion.2
  82.4 1.4 fusion.89
  83.8 1.7 %fusion.88 = f32[512,1024]{0,1:T(8,128)S(1)} fusion(bf16[64,1024]{1,0:T(8,128)(2,1)S(1)} %get-tuple-element.270, s32[512]{0:T(512)S(1)} %add_select_fusion.2, bf16[16,512,64]{1,2,0:T(8,128)(2,1)} %get-tuple-element.269, s32[]{:T(128)S(6)} %copy.50), kind=kOutput, calls=%fused_computation.5.clone.1 | convolution fusion | flops 100958208 | bytes 2295812 | tf_op jit(solution)/shard_map/while/body/eval_jaxpr/dot_general | solution.py:13
  85.5 0.3 multiply_reduce_fusion.2
  85.9 1.4 fusion.89
  87.3 1.7 %fusion.88 = f32[512,1024]{0,1:T(8,128)S(1)} fusion(bf16[64,1024]{1,0:T(8,128)(2,1)S(1)} %get-tuple-element.270, s32[512]{0:T(512)S(1)} %add_select_fusion.2, bf16[16,512,64]{1,2,0:T(8,128)(2,1)} %get-tuple-element.269, s32[]{:T(128)S(6)} %copy.50), kind=kOutput, calls=%fused_computation.5.clone.1 | convolution fusion | flops 100958208 | bytes 2295812 | tf_op jit(solution)/shard_map/while/body/eval_jaxpr/dot_general | solution.py:13
  89.4 1.4 fusion.89
  90.9 1.7 %fusion.88 = f32[512,1024]{0,1:T(8,128)S(1)} fusion(bf16[64,1024]{1,0:T(8,128)(2,1)S(1)} %get-tuple-element.270, s32[512]{0:T(512)S(1)} %add_select_fusion.2, bf16[16,512,64]{1,2,0:T(8,128)(2,1)} %get-tuple-element.269, s32[]{:T(128)S(6)} %copy.50), kind=kOutput, calls=%fused_computation.5.clone.1 | convolution fusion | flops 100958208 | bytes 2295812 | tf_op jit(solution)/shard_map/while/body/eval_jaxpr/dot_general | solution.py:13
  92.6 0.3 multiply_reduce_fusion.2
  93.0 1.4 fusion.89
  94.4 1.7 %fusion.88 = f32[512,1024]{0,1:T(8,128)S(1)} fusion(bf16[64,1024]{1,0:T(8,128)(2,1)S(1)} %get-tuple-element.270, s32[512]{0:T(512)S(1)} %add_select_fusion.2, bf16[16,512,64]{1,2,0:T(8,128)(2,1)} %get-tuple-element.269, s32[]{:T(128)S(6)} %copy.50), kind=kOutput, calls=%fused_computation.5.clone.1 | convolution fusion | flops 100958208 | bytes 2295812 | tf_op jit(solution)/shard_map/while/body/eval_jaxpr/dot_general | solution.py:13
  96.1 0.3 multiply_reduce_fusion.2
  96.5 1.4 fusion.89
  97.9 1.7 %fusion.88 = f32[512,1024]{0,1:T(8,128)S(1)} fusion(bf16[64,1024]{1,0:T(8,128)(2,1)S(1)} %get-tuple-element.270, s32[512]{0:T(512)S(1)} %add_select_fusion.2, bf16[16,512,64]{1,2,0:T(8,128)(2,1)} %get-tuple-element.269, s32[]{:T(128)S(6)} %copy.50), kind=kOutput, calls=%fused_computation.5.clone.1 | convolution fusion | flops 100958208 | bytes 2295812 | tf_op jit(solution)/shard_map/while/body/eval_jaxpr/dot_general | solution.py:13
  99.6 0.3 multiply_reduce_fusion.2
  100.0 1.4 fusion.89
  101.4 1.7 %fusion.88 = f32[512,1024]{0,1:T(8,128)S(1)} fusion(bf16[64,1024]{1,0:T(8,128)(2,1)S(1)} %get-tuple-element.270, s32[512]{0:T(512)S(1)} %add_select_fusion.2, bf16[16,512,64]{1,2,0:T(8,128)(2,1)} %get-tuple-element.269, s32[]{:T(128)S(6)} %copy.50), kind=kOutput, calls=%fused_computation.5.clone.1 | convolution fusion | flops 100958208 | bytes 2295812 | tf_op jit(solution)/shard_map/while/body/eval_jaxpr/dot_general | solution.py:13
  103.1 0.3 multiply_reduce_fusion.2
  103.5 1.4 fusion.89
  104.9 6.9 %all-to-all-start.2 = ((bf16[16,512,64]{1,2,0:T(8,128)(2,1)}), bf16[16,512,64]{1,2,0:T(8,128)(2,1)S(1)}, u32[]{:S(2)}, u32[]{:S(2)}) async-start(bf16[16,512,64]{1,2,0:T(8,128)(2,1)} %get-tuple-element.119), calls=%async_computation.2 | async-start | bytes 2097152 | tf_op jit(solution)/shard_map/all_to_all | solution.py:96
  111.8 1.9 %multiply_convert_fusion.1 = bf16[256,512]{1,0:T(8,128)(2,1)S(1)} fusion(bf16[4,512,512]{2,1,0:T(8,128)(2,1)} %param.36, bf16[256,512]{1,0:T(8,128)(2,1)S(1)} %multiply_convert_fusion.4, bf16[256,512]{1,0:T(8,128)(2,1)S(1)} %copy-done.2), kind=kOutput, calls=%fused_computation.54 | convolution fusion | flops 271450112 | bytes 2359296 | tf_op jit(solution)/shard_map/dot_general | solution.py:13
  113.7 1.9 %fusion.25 = f32[256,512]{1,0:T(8,128)S(1)} fusion(bf16[4,512,512]{2,1,0:T(8,128)(2,1)} %param.36, bf16[256,512]{1,0:T(8,128)(2,1)S(1)} %multiply_convert_fusion.1), kind=kOutput, calls=%fused_computation.42 | convolution fusion | flops 269090816 | bytes 1835008 | tf_op jit(solution)/shard_map/dot_general | solution.py:13
  115.6 19.0 %all-to-all-done.2 = bf16[16,512,64]{1,2,0:T(8,128)(2,1)S(1)} async-done(((bf16[16,512,64]{1,2,0:T(8,128)(2,1)}), bf16[16,512,64]{1,2,0:T(8,128)(2,1)S(1)}, u32[]{:S(2)}, u32[]{:S(2)}) %all-to-all-start.2) | async-done | bytes 1048608 | tf_op jit(solution)/shard_map/all_to_all | solution.py:96
  134.8 0.8 copy-done.16
  135.6 2.0 %add_convert_fusion = bf16[256,512]{1,0:T(8,128)(2,1)S(1)} fusion(bf16[64,512]{1,0:T(8,128)(2,1)S(1)} %copy-done.10, bf16[8192,64]{0,1:T(8,128)(2,1)S(1)} %bitcast.85, s32[8192]{0:T(1024)S(1)} %copy-done.12, f32[256,512]{1,0:T(8,128)S(1)} %fusion.25, bf16[256,512]{1,0:T(8,128)(2,1)S(1)} %copy-done.16), kind=kOutput, calls=%fused_computation.50 | convolution fusion | flops 289030144 | bytes 2195456 | tf_op jit(solution)/shard_map/dot_general | solution.py:13
  137.7 1.0 add_convert_fusion.1
  (121 shorter events, 3.4 us)
Async XLA Ops:
  0.6 9.2 %copy-start = (bf16[512,512]{1,0:T(8,128)(2,1)S(1)}, bf16[512,512]{1,0:T(8,128)(2,1)}, u32[]{:S(2)}) copy-start(bf16[512,512]{1,0:T(8,128)(2,1)} %param.31) | copy-start | bytes 1572868
  2.3 15.9 %copy-start.9 = (bf16[512,64]{0,1:T(8,128)(2,1)S(1)}, bf16[512,64]{0,1:T(8,128)(2,1)}, u32[]{:S(2)}) copy-start(bf16[512,64]{0,1:T(8,128)(2,1)} %param.33) | copy-start | bytes 196612
  2.3 15.9 %copy-start.11 = (s32[8192]{0:T(1024)S(1)}, s32[8192]{0:T(1024)}, u32[]{:S(2)}) copy-start(s32[8192]{0:T(1024)} %param.25) | copy-start | bytes 98308
  2.3 14.4 %all-to-all-start = ((bf16[16,8,256]{2,1,0:T(8,128)(2,1)}), bf16[16,8,256]{2,1,0:T(8,128)(2,1)S(1)}, u32[]{:S(2)}, u32[]{:S(2)}) async-start(bf16[16,8,256]{2,1,0:T(8,128)(2,1)} %fusion.21), calls=%async_computation | async-start | bytes 131072 | tf_op jit(solution)/shard_map/all_to_all | solution.py:83
  20.0 5.6 %copy-start.4 = (s32[8192]{0:T(1024)S(1)}, s32[8192]{0:T(1024)}, u32[]{:S(2)}) copy-start(s32[8192]{0:T(1024)} %param.27) | copy-start | bytes 98308
  20.1 5.6 %copy-start.5 = (s32[8192]{0:T(1024)S(1)}, s32[8192]{0:T(1024)}, u32[]{:S(2)}) copy-start(s32[8192]{0:T(1024)} %param.26) | copy-start | bytes 98308
  20.1 5.7 %copy-start.3 = (bf16[16,8192]{1,0:T(8,128)(2,1)S(1)}, bf16[16,8192]{1,0:T(8,128)(2,1)}, u32[]{:S(2)}) copy-start(bf16[16,8192]{1,0:T(8,128)(2,1)} %param.29) | copy-start | bytes 786436
  21.2 4.8 %copy-start.6 = (s32[8192]{0:T(1024)S(1)}, s32[8192]{0:T(1024)}, u32[]{:S(2)}) copy-start(s32[8192]{0:T(1024)} %param.28) | copy-start | bytes 98308
  21.2 27.4 %copy-start.1 = (bf16[64,1024]{1,0:T(8,128)(2,1)S(1)}, bf16[64,1024]{1,0:T(8,128)(2,1)}, u32[]{:S(2)}) copy-start(bf16[64,1024]{1,0:T(8,128)(2,1)} %param.34) | copy-start | bytes 393220
  21.2 27.4 %all-to-all-start.1 = ((bf16[16,512,64]{1,2,0:T(8,128)(2,1)}), bf16[16,512,64]{1,2,0:T(8,128)(2,1)}, u32[]{:S(2)}, u32[]{:S(2)}) async-start(bf16[16,512,64]{1,2,0:T(8,128)(2,1)} %bitcast.66), calls=%async_computation.1 | async-start | bytes 2097152 | tf_op jit(solution)/shard_map/all_to_all | solution.py:90
  104.9 6.9 %copy-start.2 = (bf16[256,512]{1,0:T(8,128)(2,1)S(1)}, bf16[256,512]{1,0:T(8,128)(2,1)}, u32[]{:S(2)}) copy-start(bf16[256,512]{1,0:T(8,128)(2,1)} %param.20) | copy-start | bytes 786436
  104.9 29.8 %all-to-all-start.2 = ((bf16[16,512,64]{1,2,0:T(8,128)(2,1)}), bf16[16,512,64]{1,2,0:T(8,128)(2,1)S(1)}, u32[]{:S(2)}, u32[]{:S(2)}) async-start(bf16[16,512,64]{1,2,0:T(8,128)(2,1)} %get-tuple-element.119), calls=%async_computation.2 | async-start | bytes 2097152 | tf_op jit(solution)/shard_map/all_to_all | solution.py:96
  113.7 1.9 %copy-start.15 = (bf16[256,512]{1,0:T(8,128)(2,1)}, bf16[256,512]{1,0:T(8,128)(2,1)S(1)}, u32[]{:S(2)}) copy-start(bf16[256,512]{1,0:T(8,128)(2,1)S(1)} %multiply_convert_fusion.1) | copy-start | bytes 786436
  115.6 19.2 %copy-start.10 = (bf16[64,512]{1,0:T(8,128)(2,1)S(1)}, bf16[64,512]{1,0:T(8,128)(2,1)}, u32[]{:S(2)}) copy-start(bf16[64,512]{1,0:T(8,128)(2,1)} %param.35) | copy-start | bytes 196612
  115.6 19.2 %copy-start.12 = (s32[8192]{0:T(1024)S(1)}, s32[8192]{0:T(1024)}, u32[]{:S(2)}) copy-start(s32[8192]{0:T(1024)} %param.30) | copy-start | bytes 98308
  134.7 1.0 copy-start.16
  135.6 2.0 %copy-start.7 = (bf16[16,256]{1,0:T(8,128)(2,1)S(1)}, bf16[16,256]{1,0:T(8,128)(2,1)}, u32[]{:S(2)}) copy-start(bf16[16,256]{1,0:T(8,128)(2,1)} %param.21) | copy-start | bytes 24580
  135.6 2.0 %copy-start.8 = (bf16[512,256]{1,0:T(8,128)(2,1)S(1)}, bf16[512,256]{1,0:T(8,128)(2,1)}, u32[]{:S(2)}) copy-start(bf16[512,256]{1,0:T(8,128)(2,1)} %param.37) | copy-start | bytes 786436
  135.6 2.0 %copy-start.13 = (s32[256]{0:T(256)S(1)}, s32[256]{0:T(256)}, u32[]{:S(2)}) copy-start(s32[256]{0:T(256)} %param.24) | copy-start | bytes 3076
  137.7 1.0 copy-start.14
where the time goes:
time: 141 us; the launch traced here: 139 us
  matrix products  61.6 us (44%)
  waiting for transfers between devices  47.2 us (33%)
  starting transfers between devices  18.9 us (13%)
  other arithmetic  4.89 us (3%)
  local copies, waits for them, and re-layouts  4.5 us (3%)
    dot_general x24, matrix products, matmul(): return jnp.dot(left, right, preferred_element_type=jnp.float32)  39.5 us
    all_to_all x1, waiting for transfers between devices, on_device(): lax.all_to_all(pick_rows(send_edges, projected), 'graph', split_axis=0, c...  22.6 us
    dot_general x16, matrix products, one_block(): jnp.dot(out_hot, mixed, precision=lax.Precision.HIGHEST, preferred_elemen...  22 us
    all_to_all x1, waiting for transfers between devices, on_device(): lax.all_to_all(slot_sums, 'graph', split_axis=0, concat_axis=0, tiled=True)  19 us
    all_to_all x1, starting transfers between devices, on_device(): lax.all_to_all(pick_rows(atom_sends, atom_state), 'graph', split_axis=0,...  7.52 us
    all_to_all x1, starting transfers between devices, on_device(): lax.all_to_all(slot_sums, 'graph', split_axis=0, concat_axis=0, tiled=True)  6.87 us
    all_to_all x1, waiting for transfers between devices, on_device(): lax.all_to_all(pick_rows(atom_sends, atom_state), 'graph', split_axis=0,...  5.63 us
    while x32, other arithmetic  4.49 us
  transfers between devices with their start and end apart: 3, of which 3 were waited for; matrix products, arithmetic and copies ran while one was open for 4% of the time, Pallas kernels for 0%

commit v1 on v0

--- a/solution.py
+++ b/solution.py
@@ -1,6 +1,10 @@
+import functools
+
 import jax
 import jax.numpy as jnp
 from jax import lax
+from jax.experimental import pallas as pl
+from jax.experimental.pallas import tpu as pltpu
 from jax.sharding import PartitionSpec as P
 
 WIN = 512
@@ -58,7 +62,7 @@
     return summed.reshape(trip_count, -1).astype(jnp.bfloat16)
 
 
-def on_device(
+def plain_on_device(
     edge_state,
     atom_state,
     atom_sends,
@@ -118,6 +122,332 @@
     return (edge_out, atom_out)
 
 
+def silu(value):
+    return value / (1.0 + jnp.exp(-value))
+
+
+def dot_at(left, right, left_dim, right_dim):
+    return lax.dot_general(
+        left, right, (((left_dim,), (right_dim,)), ((), ())), preferred_element_type=jnp.float32
+    )
+
+
+def hot_columns(row_count, indices):
+    rows = lax.broadcasted_iota(jnp.int32, (row_count, indices.shape[1]), 0)
+    return jnp.where(rows == indices, 1.0, 0.0).astype(jnp.bfloat16)
+
+
+def front_kernel(
+    n,
+    atom_ref,
+    asend_ref,
+    source_ref,
+    edge_hbm,
+    ends_hbm,
+    basis_hbm,
+    w_edge_hbm,
+    w_source_hbm,
+    w_down_hbm,
+    w_res_hbm,
+    proj_ref,
+    chain_ref,
+    ends_out,
+    basis_out,
+    edge_v,
+    w_edge_v,
+    w_source_v,
+    w_down_v,
+    w_res_v,
+    atoms_out,
+    atoms_in,
+    load_sem,
+    own_sem,
+    send_sem,
+    recv_sem,
+):
+    me = lax.axis_index("graph")
+    cap = ends_out.shape[2]
+    loads = [
+        pltpu.make_async_copy(src, dst, load_sem.at[i])
+        for i, (src, dst) in enumerate(
+            (
+                (edge_hbm, edge_v),
+                (w_edge_hbm, w_edge_v),
+                (w_source_hbm, w_source_v),
+                (w_down_hbm, w_down_v),
+                (w_res_hbm, w_res_v),
+            )
+        )
+    ]
+    for load in loads:
+        load.start()
+
+    barrier = pltpu.get_barrier_semaphore()
+    for step in range(1, n):
+        pl.semaphore_signal(
+            barrier,
+            inc=1,
+            device_id={"graph": lax.rem(me + step, n)},
+            device_id_type=pl.DeviceIdType.MESH,
+        )
+    picked = dot_at(hot_columns(atom_ref.shape[0], asend_ref[...]), atom_ref[...], 0, 0)
+    atoms_out[...] = picked.reshape(atoms_out.shape).astype(jnp.bfloat16)
+    pl.semaphore_wait(barrier, n - 1)
+
+    def parts(peer):
+        lanes = pl.ds(pl.multiple_of(peer * cap, cap), cap)
+        return (
+            (atoms_out.at[peer], atoms_in.at[me]),
+            (ends_hbm.at[peer], ends_out.at[me]),
+            (basis_hbm.at[:, lanes], basis_out.at[me]),
+        )
+
+    remote = [[], [], []]
+    local = []
+    for kind in range(3):
+        for step in range(1, n):
+            peer = lax.rem(me + step, n)
+            src, dst = parts(peer)[kind]
+            copy = pltpu.make_async_remote_copy(
+                src_ref=src,
+                dst_ref=dst,
+                send_sem=send_sem.at[kind, step],
+                recv_sem=recv_sem.at[kind, step],
+                device_id={"graph": peer},
+                device_id_type=pl.DeviceIdType.MESH,
+            )
+            copy.start()
+            remote[kind].append(copy)
+        src, dst = parts(me)[kind]
+        copy = pltpu.make_async_copy(src, dst, own_sem.at[kind])
+        copy.start()
+        local.append(copy)
+
+    loads[0].wait()
+    loads[1].wait()
+    edge = edge_v[...]
+    pre_act = matmul(edge, w_edge_v[...])
+    pick = hot_columns(atoms_in.shape[0] * atoms_in.shape[1], source_ref[...])
+    loads[2].wait()
+    loads[3].wait()
+    for copy in remote[0]:
+        copy.wait_recv()
+    local[0].wait()
+    arrived = atoms_in[...].astype(jnp.float32).reshape(pick.shape[0], -1).astype(jnp.bfloat16)
+    src_rows = dot_at(pick, arrived, 0, 0).astype(jnp.bfloat16)
+    activated = silu(pre_act + matmul(src_rows, w_source_v[...])).astype(jnp.bfloat16)
+    proj_ref[...] = silu(matmul(activated, w_down_v[...])).astype(jnp.bfloat16)
+    loads[4].wait()
+    base = ((edge.astype(jnp.float32) + activated.astype(jnp.float32)) * inv_root).astype(
+        jnp.bfloat16
+    )
+    inner_one = silu(matmul(base, w_res_v[0])).astype(jnp.bfloat16)
+    middle = ((base.astype(jnp.float32) + silu(matmul(inner_one, w_res_v[1]))) * inv_root).astype(
+        jnp.bfloat16
+    )
+    inner_two = silu(matmul(middle, w_res_v[2])).astype(jnp.bfloat16)
+    chain_ref[...] = (middle.astype(jnp.float32) + silu(matmul(inner_two, w_res_v[3]))) * inv_root
+    for kind in (1, 2):
+        for copy in remote[kind]:
+            copy.wait_recv()
+        local[kind].wait()
+    for kind in range(3):
+        for copy in remote[kind]:
+            copy.wait_send()
+
+
+def look_up(table, indices):
+    width = 128
+    found = []
+    for start in range(0, indices.shape[1], width):
+        wanted = indices[:, start : start + width]
+        lane = lax.rem(wanted, width)
+        chunk_of = wanted // width
+        value = jnp.zeros_like(wanted)
+        for chunk in range(table.shape[1] // width):
+            part = jnp.take_along_axis(
+                table[:, chunk * width : (chunk + 1) * width], lane, axis=1, mode="promise_in_bounds"
+            )
+            value = jnp.where(chunk_of == chunk, part, value)
+        found.append(value)
+    return jnp.concatenate(found, axis=1)
+
+
+def triplet_kernel(
+    n,
+    proj_ref,
+    chain_ref,
+    ends_ref,
+    basis_ref,
+    send_ref,
+    return_ref,
+    target_ref,
+    atom_ref,
+    w_bilinear_ref,
+    w_up_ref,
+    w_atom_ref,
+    edge_out_ref,
+    atom_out_ref,
+    table_v,
+    in_v,
+    out_v,
+    expand_v,
+    sum_v,
+):
+    edge_count, width = proj_ref.shape
+    basis_count, cap = basis_ref.shape[1:]
+    table_v[...] = dot_at(w_bilinear_ref[...], proj_ref[...], 0, 1).astype(jnp.bfloat16)
+    for start in range(0, n, 8):
+        some = slice(start, start + 8)
+        in_v[some] = look_up(send_ref[some], ends_ref[some, 0, :])
+        out_v[some] = look_up(return_ref[some], ends_ref[some, 1, :])
+    sum_v[...] = jnp.zeros_like(sum_v)
+
+    def one_tile(tile, carry):
+        expand_v[...] = matmul(table_v[...], hot_columns(edge_count, in_v[pl.ds(tile, 1), :]))
+        coeffs = basis_ref[tile].astype(jnp.float32)
+        mixed = jnp.zeros((width, cap), jnp.float32)
+        for k in range(basis_count):
+            mixed = mixed + coeffs[k : k + 1, :] * expand_v[k * width : (k + 1) * width, :]
+        out_hot = hot_columns(edge_count, out_v[pl.ds(tile, 1), :])
+        sum_v[...] += dot_at(mixed.astype(jnp.bfloat16), out_hot, 1, 1)
+        return carry
+
+    lax.fori_loop(0, n, one_tile, 0, unroll=2)
+    aggregate = sum_v[...].T.astype(jnp.bfloat16)
+    update = silu(matmul(aggregate, w_up_ref[...]))
+    edge_out = (chain_ref[...] + update).astype(jnp.bfloat16)
+    edge_out_ref[...] = edge_out
+    contrib = matmul(edge_out, w_atom_ref[...]).astype(jnp.bfloat16)
+    atom_sum = matmul(hot_columns(atom_ref.shape[0], target_ref[...]), contrib)
+    atom_out_ref[...] = (atom_ref[...].astype(jnp.float32) + silu(0.25 * atom_sum)).astype(
+        jnp.bfloat16
+    )
+
+
+def on_device(
+    n,
+    edge_state,
+    atom_state,
+    atom_sends,
+    edge_source,
+    edge_target,
+    send_edges,
+    triplet_in,
+    triplet_out,
+    triplet_valid,
+    triplet_basis,
+    return_edges,
+    w_edge,
+    w_source,
+    w_down,
+    w_bilinear,
+    w_up,
+    w_residual,
+    w_atom,
+):
+    cap = triplet_in.shape[0] // n
+    if cap % WIN or n % 8:
+        return plain_on_device(
+            edge_state,
+            atom_state,
+            atom_sends,
+            edge_source,
+            edge_target,
+            send_edges,
+            triplet_in,
+            triplet_out,
+            triplet_valid,
+            triplet_basis,
+            return_edges,
+            w_edge,
+            w_source,
+            w_down,
+            w_bilinear,
+            w_up,
+            w_residual,
+            w_atom,
+        )
+    edge_count, edge_width = edge_state.shape
+    atom_count, atom_width = atom_state.shape
+    basis_count = triplet_basis.shape[0]
+    width = w_down.shape[1]
+    slots = atom_sends.shape[0] // n
+    ends = jnp.stack(
+        [(triplet_in % cap).reshape(n, cap), (triplet_out % cap).reshape(n, cap)], axis=1
+    )
+    basis = triplet_basis * triplet_valid.astype(triplet_basis.dtype)[None, :]
+    vmem = pl.BlockSpec(memory_space=pltpu.VMEM)
+    hbm = pl.BlockSpec(memory_space=pl.ANY)
+    bf16 = jnp.bfloat16
+    projected, chain, my_ends, my_basis = pl.pallas_call(
+        functools.partial(front_kernel, n),
+        out_shape=(
+            jax.ShapeDtypeStruct((edge_count, width), bf16),
+            jax.ShapeDtypeStruct((edge_count, edge_width), jnp.float32),
+            jax.ShapeDtypeStruct((n, 2, cap), jnp.int32),
+            jax.ShapeDtypeStruct((n, basis_count, cap), bf16),
+        ),
+        in_specs=[vmem] * 3 + [hbm] * 7,
+        out_specs=(vmem, vmem, vmem, vmem),
+        scratch_shapes=[
+            pltpu.VMEM(edge_state.shape, bf16),
+            pltpu.VMEM(w_edge.shape, bf16),
+            pltpu.VMEM(w_source.shape, bf16),
+            pltpu.VMEM(w_down.shape, bf16),
+            pltpu.VMEM(w_residual.shape, bf16),
+            pltpu.VMEM((n, slots, atom_width), bf16),
+            pltpu.VMEM((n, slots, atom_width), bf16),
+            pltpu.SemaphoreType.DMA((5,)),
+            pltpu.SemaphoreType.DMA((3,)),
+            pltpu.SemaphoreType.DMA((3, n)),
+            pltpu.SemaphoreType.DMA((3, n)),
+        ],
+        compiler_params=pltpu.CompilerParams(collective_id=0, has_side_effects=True),
+        name="front",
+    )(
+        atom_state,
+        atom_sends.reshape(1, -1),
+        edge_source.reshape(1, -1),
+        edge_state,
+        ends,
+        basis,
+        w_edge,
+        w_source,
+        w_down,
+        w_residual,
+    )
+    return pl.pallas_call(
+        functools.partial(triplet_kernel, n),
+        out_shape=(
+            jax.ShapeDtypeStruct((edge_count, edge_width), bf16),
+            jax.ShapeDtypeStruct((atom_count, atom_width), bf16),
+        ),
+        in_specs=[vmem] * 11,
+        out_specs=(vmem, vmem),
+        scratch_shapes=[
+            pltpu.VMEM((basis_count * width, edge_count), bf16),
+            pltpu.VMEM((n, cap), jnp.int32),
+            pltpu.VMEM((n, cap), jnp.int32),
+            pltpu.VMEM((basis_count * width, cap), jnp.float32),
+            pltpu.VMEM((width, edge_count), jnp.float32),
+        ],
+        name="triplets",
+    )(
+        projected,
+        chain,
+        my_ends,
+        my_basis,
+        send_edges.reshape(n, cap),
+        return_edges.reshape(n, cap),
+        edge_target.reshape(1, -1),
+        atom_state,
+        w_bilinear,
+        w_up,
+        w_atom,
+    )
+
+
 def solution(mesh):
     placed = (
         P(("groups", "graph"), None),
@@ -140,7 +470,7 @@
         P(),
     )
     return jax.shard_map(
-        on_device,
+        functools.partial(on_device, mesh.shape["graph"]),
         mesh=mesh,
         in_specs=placed,
         out_specs=(P(("groups", "graph"), None), P(("groups", "graph"), None)),

time: 141 us -> 37 us (0.26); the launches traced: 139 us -> 36.6 us
  matrix products: 61.6 us -> 0 us
  waiting for transfers between devices: 47.2 us -> 0 us
  Pallas kernels: 0 us -> 28.4 us
  starting transfers between devices: 18.9 us -> 0 us
  local copies, waits for them, and re-layouts: 4.5 us -> 2.84 us
    dot_general x40 -> x0, matrix products: 61.6 us -> none  [the longest x24 39.5 us: matmul(): return jnp.dot(left, right, preferred_element_type=jnp.float32)]
    all_to_all x3 -> x0, waiting for transfers between devices: 47.2 us -> none  [the longest x1 22.6 us: on_device(): lax.all_to_all(pick_rows(send_edges, projected), 'graph', split_axis=0, c...]
    pallas_call x0 -> x2, Pallas kernels: none -> 28.4 us  [the longest x1 16.4 us: on_device(): pl.pallas_call(functools.partial(front_kernel, n), out_shape=(jax.ShapeDt...]
    all_to_all x3 -> x0, starting transfers between devices: 18.9 us -> none  [the longest x1 7.52 us: on_device(): lax.all_to_all(pick_rows(atom_sends, atom_state), 'graph', split_axis=0,...]
    while x32 -> x0, other arithmetic: 4.49 us -> none
    dot_general x16 -> x0, local copies, waits for them, and re-layouts: 1.95 us -> none  [bilinear_terms(): mixed = jnp.einsum('tkd,kt->td', expanded, coeffs.astype(jnp.float32))]
    mul x0 -> x1, other arithmetic: none -> 1.68 us  [on_device(): basis = triplet_basis * triplet_valid.astype(triplet_basis.dtype)[None, :]]
  transfers between devices with their start and end apart: 3 -> 0, of which waited for: 3 -> 0; matrix products, arithmetic and copies ran while one was open for 4% -> 0% of each run, Pallas kernels for 0% -> 0%
where the time goes in v1:
time: 37 us; the launch traced here: 36.6 us
  Pallas kernels  28.4 us (77%)
  other arithmetic  4.67 us (13%)
  local copies, waits for them, and re-layouts  2.84 us (8%)
  between operations  0.66 us (2%)
    pallas_call x1, Pallas kernels, on_device(): pl.pallas_call(functools.partial(front_kernel, n), out_shape=(jax.ShapeDt...  16.4 us
    pallas_call x1, Pallas kernels, on_device(): pl.pallas_call(functools.partial(triplet_kernel, n), out_shape=(jax.Shape...  12 us
    mul x1, other arithmetic, on_device(): basis = triplet_basis * triplet_valid.astype(triplet_basis.dtype)[None, :]  1.68 us
    unnamed x5, local copies, waits for them, and re-layouts  1.6 us
    select_n x1, other arithmetic, on_device(): triplet_out % cap  0.78 us
    select_n x1, other arithmetic, on_device(): triplet_in % cap  0.77 us
    convert_element_type x1, other arithmetic, on_device(): basis = triplet_basis * triplet_valid.astype(triplet_basis.dtype)[None, :]  0.76 us

profile of v1, /device:TPU:0, one launch (start us, length us, event | category | flops | bytes accessed | tf_op | source)
XLA Modules:
  0.0 36.6 jit_solution(3268130929477877716)
XLA Ops:
  0.6 0.8 %convert_element_type.3 = bf16[8192]{0:T(1024)(128)(2,1)S(1)} convert(s32[8192]{0:T(1024)} %param.26) | non-fusion elementwise | flops 8192 | bytes 49152 | tf_op jit(solution)/shard_map/convert_element_type | solution.py:379
  1.4 1.7 %broadcast_multiply_fusion.basis_hbm = bf16[16,8192]{1,0:T(8,128)(2,1)} fusion(bf16[16,8192]{1,0:T(8,128)(2,1)} %param.27, bf16[8192]{0:T(1024)(128)(2,1)S(1)} %convert_element_type.3), kind=kLoop, calls=%fused_computation | loop fusion | flops 131072 | bytes 540672 | tf_op jit(solution)/shard_map/mul | solution.py:379
  3.1 0.0 copy-start
  3.1 0.0 copy-start.1
  3.1 1.6 %copy.20.w_down_hbm = bf16[512,64]{1,0:T(8,128)(2,1)} copy(bf16[512,64]{0,1:T(8,128)(2,1)} %param.31) | data formatting | bytes 131072 | tf_op args[13]
  4.7 0.8 %add_select_fusion.1 = s32[8192]{0:T(1024)S(1)} fusion(s32[8192]{0:T(1024)} %param.24), kind=kLoop, calls=%fused_computation.5 | loop fusion | flops 90112 | bytes 65536 | tf_op jit(solution)/shard_map/jit(remainder)/select_n | solution.py:377
  5.5 0.8 %add_select_fusion = s32[8192]{0:T(1024)S(1)} fusion(s32[8192]{0:T(1024)} %param.25), kind=kLoop, calls=%fused_computation.2 | loop fusion | flops 90112 | bytes 65536 | tf_op jit(solution)/shard_map/jit(remainder)/select_n | solution.py:377
  6.2 0.7 %pad_add_fusion.ends_hbm = s32[16,2,512]{2,1,0:T(2,128)} fusion(s32[16,1,512]{2,1,0:T(1,128)S(1)} %bitcast.6, s32[16,1,512]{2,1,0:T(1,128)S(1)} %bitcast.5), kind=kLoop, calls=%fused_computation.1 | loop fusion | flops 16384 | bytes 131072 | tf_op jit(solution)/shard_map/stack | solution.py:376
  6.9 16.4 %front.1 = (bf16[256,64]{1,0:T(8,128)(2,1)}, f32[256,512]{1,0:T(8,128)}, s32[16,2,512]{2,1,0:T(2,128)}, bf16[16,16,512]{2,1,0:T(8,128)(2,1)}) custom-call(bf16[16,256]{1,0:T(8,128)(2,1)} %atom_ref.3, s32[1,128]{1,0:T(1,128)} %bitcast.9, s32[1,256]{1,0:T(1,128)} %bitcast.7, bf16[256,512]{1,0:T(8,128)(2,1)} %edge_hbm.1, s32[16,2,512]{2,1,0:T(2,128)} %pad_add_fusion.ends_hbm, ...), custom_call_target="tpu_custom_call" | custom-call | tf_op jit(solution)/shard_map/front/pallas_call | solution.py:383
  23.3 0.0 copy-done
  23.3 0.6 %reshape.22.send_ref = s32[16,512]{1,0:T(8,128)} reshape(s32[8192]{0:T(1024)S(1)} %copy-done) | data formatting | bytes 65536 | tf_op jit(solution)/shard_map/reshape | solution.py:441
  23.9 0.0 copy-done.1
  23.9 0.6 %reshape.23.return_ref = s32[16,512]{1,0:T(8,128)} reshape(s32[8192]{0:T(1024)S(1)} %copy-done.1) | data formatting | bytes 65536 | tf_op jit(solution)/shard_map/reshape | solution.py:442
  24.6 12.0 %triplets.1 = (bf16[256,512]{1,0:T(8,128)(2,1)}, bf16[16,256]{1,0:T(8,128)(2,1)}) custom-call(bf16[256,64]{1,0:T(8,128)(2,1)} %get-tuple-element.6.proj_ref, f32[256,512]{1,0:T(8,128)} %get-tuple-element.7.chain_ref, s32[16,2,512]{2,1,0:T(2,128)} %get-tuple-element.8.ends_ref, bf16[16,16,512]{2,1,0:T(8,128)(2,1)} %get-tuple-element.9.basis_ref, ...), custom_call_target="tpu_custom_call" | custom-call | tf_op jit(solution)/shard_map/triplets/pallas_call | solution.py:420
Async XLA Ops:
  3.1 20.2 %copy-start = (s32[8192]{0:T(1024)S(1)}, s32[8192]{0:T(1024)}, u32[]{:S(2)}) copy-start(s32[8192]{0:T(1024)} %param.23) | copy-start | bytes 98308
  3.1 20.9 %copy-start.1 = (s32[8192]{0:T(1024)S(1)}, s32[8192]{0:T(1024)}, u32[]{:S(2)}) copy-start(s32[8192]{0:T(1024)} %param.28) | copy-start | bytes 98308

commit v2 on v0

--- a/solution.py
+++ b/solution.py
@@ -1,6 +1,10 @@
+import functools
+
 import jax
 import jax.numpy as jnp
 from jax import lax
+from jax.experimental import pallas as pl
+from jax.experimental.pallas import tpu as pltpu
 from jax.sharding import PartitionSpec as P
 
 WIN = 512
@@ -58,7 +62,7 @@
     return summed.reshape(trip_count, -1).astype(jnp.bfloat16)
 
 
-def on_device(
+def plain_on_device(
     edge_state,
     atom_state,
     atom_sends,
@@ -118,6 +122,313 @@
     return (edge_out, atom_out)
 
 
+def silu(value):
+    return value / (1.0 + jnp.exp(-value))
+
+
+def dot_at(left, right, left_dim, right_dim):
+    return lax.dot_general(
+        left, right, (((left_dim,), (right_dim,)), ((), ())), preferred_element_type=jnp.float32
+    )
+
+
+def hot_columns(row_count, indices):
+    rows = lax.broadcasted_iota(jnp.int32, (row_count, indices.shape[1]), 0)
+    return jnp.where(rows == indices, 1.0, 0.0).astype(jnp.bfloat16)
+
+
+def partner(me, step, n):
+    peer = me
+    bit = 1
+    while bit < n:
+        mine = lax.rem(lax.div(me, bit), 2)
+        flip = (step // bit) % 2 if isinstance(step, int) else lax.rem(lax.div(step, bit), 2)
+        peer = peer + flip * (1 - 2 * mine) * bit
+        bit *= 2
+    return peer
+
+
+def look_up(table, indices):
+    lanes = 128
+    found = []
+    for start in range(0, indices.shape[1], lanes):
+        wanted = jnp.broadcast_to(indices[:, start : start + lanes], (8, lanes))
+        lane = wanted & (lanes - 1)
+        value = jnp.zeros_like(wanted)
+        for first in range(0, table.shape[1], lanes):
+            part = jnp.take_along_axis(
+                jnp.broadcast_to(table[:, first : first + lanes], (8, lanes)),
+                lane,
+                axis=1,
+                mode="promise_in_bounds",
+            )
+            value = jnp.where(wanted - lane == first, part, value)
+        found.append(value)
+    return jnp.concatenate(found, axis=1)
+
+
+def hot_from(row_count, eight_rows):
+    rows = lax.broadcasted_iota(jnp.int32, (row_count, eight_rows.shape[1]), 0)
+    spread = jnp.concatenate([eight_rows] * (row_count // 8), axis=0)
+    return jnp.where(rows == spread, 1.0, 0.0).astype(jnp.bfloat16)
+
+
+def block_kernel(n, loaded, *refs):
+    sources = refs[:loaded]
+    in_hbm, out_hbm, valid_hbm, basis_hbm = refs[loaded : loaded + 4]
+    edge_out_ref, atom_out_ref = refs[loaded + 4 : loaded + 6]
+    held = refs[loaded + 6 : 2 * loaded + 6]
+    (
+        in_v,
+        out_v,
+        valid_v,
+        basis_v,
+        atoms_out,
+        atoms_in,
+        chain_v,
+        table_v,
+        expand_v,
+        sum_v,
+        load_sem,
+        send_sem,
+        recv_sem,
+    ) = refs[2 * loaded + 6 :]
+    (
+        atom_v,
+        asend_v,
+        edge_v,
+        w_edge_v,
+        source_v,
+        w_source_v,
+        w_down_v,
+        w_bilinear_v,
+        w_res_v,
+        send_v,
+        return_v,
+        target_v,
+        w_up_v,
+        w_atom_v,
+    ) = held
+    me = lax.axis_index("graph")
+    cap = in_v.shape[2]
+    edge_count = edge_v.shape[0]
+    width = w_down_v.shape[0]
+    basis_count = basis_v.shape[1]
+
+    barrier = pltpu.get_barrier_semaphore()
+    for step in range(1, n):
+        pl.semaphore_signal(
+            barrier,
+            inc=1,
+            device_id={"graph": partner(me, step, n)},
+            device_id_type=pl.DeviceIdType.MESH,
+        )
+    loads = [
+        pltpu.make_async_copy(src, dst, load_sem.at[i])
+        for i, (src, dst) in enumerate(zip(sources, held))
+    ]
+    for load in loads:
+        load.start()
+    loads[0].wait()
+    loads[1].wait()
+    picked = dot_at(hot_columns(atom_v.shape[0], asend_v[...]), atom_v[...], 0, 0)
+    atoms_out[...] = picked.reshape(atoms_out.shape).astype(jnp.bfloat16)
+    pl.semaphore_wait(barrier, n - 1)
+
+    def parts(peer):
+        lanes = pl.ds(pl.multiple_of(peer * cap, cap), cap)
+        return (
+            (atoms_out.at[peer], atoms_in.at[me]),
+            (in_hbm.at[peer], in_v.at[me]),
+            (out_hbm.at[peer], out_v.at[me]),
+            (valid_hbm.at[peer], valid_v.at[me]),
+            (basis_hbm.at[:, lanes], basis_v.at[me]),
+        )
+
+    sent = []
+    for kinds in ((0,), (1, 2, 3, 4)):
+        for step in range(n):
+            peer = partner(me, step, n)
+            for kind in kinds:
+                src, dst = parts(peer)[kind]
+                if step == 0:
+                    copy = pltpu.make_async_copy(src, dst, recv_sem.at[kind, step])
+                else:
+                    copy = pltpu.make_async_remote_copy(
+                        src_ref=src,
+                        dst_ref=dst,
+                        send_sem=send_sem.at[kind, step],
+                        recv_sem=recv_sem.at[kind, step],
+                        device_id={"graph": peer},
+                        device_id_type=pl.DeviceIdType.MESH,
+                    )
+                    sent.append(copy)
+                copy.start()
+
+    def arrive(kind, buffer, step, peer):
+        pltpu.make_async_copy(buffer.at[peer], buffer.at[peer], recv_sem.at[kind, step]).wait()
+
+    for load in loads[2:7]:
+        load.wait()
+    edge = edge_v[...]
+    pre_act = matmul(edge, w_edge_v[...])
+    pick = hot_columns(atoms_in.shape[0] * atoms_in.shape[1], source_v[...])
+    for step in range(n):
+        arrive(0, atoms_in, step, partner(me, step, n))
+    arrived = atoms_in[...].astype(jnp.float32).reshape(pick.shape[0], -1).astype(jnp.bfloat16)
+    src_rows = dot_at(pick, arrived, 0, 0).astype(jnp.bfloat16)
+    activated = silu(pre_act + matmul(src_rows, w_source_v[...])).astype(jnp.bfloat16)
+    projected = silu(dot_at(activated, w_down_v[...], 1, 1)).astype(jnp.bfloat16)
+    for load in loads[7:]:
+        load.wait()
+    table_v[...] = dot_at(w_bilinear_v[...], projected, 0, 1).astype(jnp.bfloat16)
+    base = ((edge.astype(jnp.float32) + activated.astype(jnp.float32)) * inv_root).astype(
+        jnp.bfloat16
+    )
+    inner_one = silu(matmul(base, w_res_v[0])).astype(jnp.bfloat16)
+    middle = ((base.astype(jnp.float32) + silu(matmul(inner_one, w_res_v[1]))) * inv_root).astype(
+        jnp.bfloat16
+    )
+    inner_two = silu(matmul(middle, w_res_v[2])).astype(jnp.bfloat16)
+    chain_v[...] = (middle.astype(jnp.float32) + silu(matmul(inner_two, w_res_v[3]))) * inv_root
+    sum_v[...] = jnp.zeros_like(sum_v)
+
+    def some_tiles(group, carry):
+        tiles = []
+        for slot in range(expand_v.shape[0]):
+            step = group * expand_v.shape[0] + slot
+            tile = partner(me, step, n)
+            tiles.append(tile)
+            arrive(1, in_v, step, tile)
+            arrive(2, out_v, step, tile)
+            arrive(3, valid_v, step, tile)
+            arrive(4, basis_v, step, tile)
+        for slot, tile in enumerate(tiles):
+            in_hot = hot_from(edge_count, look_up(send_v[tile], in_v[tile] & (cap - 1)))
+            expand_v[slot] = matmul(table_v[...], in_hot)
+            coeffs = basis_v[tile].astype(jnp.float32) * valid_v[tile].astype(jnp.float32)
+            mixed = jnp.zeros((width, cap), jnp.float32)
+            for k in range(basis_count):
+                mixed = mixed + coeffs[k : k + 1, :] * expand_v[slot, k * width : (k + 1) * width, :]
+            out_hot = hot_from(edge_count, look_up(return_v[tile], out_v[tile] & (cap - 1)))
+            sum_v[...] += dot_at(mixed.astype(jnp.bfloat16), out_hot, 1, 1)
+        return carry
+
+    lax.fori_loop(0, n // expand_v.shape[0], some_tiles, 0)
+    aggregate = sum_v[...].T.astype(jnp.bfloat16)
+    update = silu(matmul(aggregate, w_up_v[...]))
+    edge_out = (chain_v[...] + update).astype(jnp.bfloat16)
+    edge_out_ref[...] = edge_out
+    contrib = matmul(edge_out, w_atom_v[...]).astype(jnp.bfloat16)
+    atom_sum = matmul(hot_columns(atom_v.shape[0], target_v[...]), contrib)
+    atom_out_ref[...] = (atom_v[...].astype(jnp.float32) + silu(0.25 * atom_sum)).astype(
+        jnp.bfloat16
+    )
+    for copy in sent:
+        copy.wait_send()
+
+
+def on_device(
+    n,
+    edge_state,
+    atom_state,
+    atom_sends,
+    edge_source,
+    edge_target,
+    send_edges,
+    triplet_in,
+    triplet_out,
+    triplet_valid,
+    triplet_basis,
+    return_edges,
+    w_edge,
+    w_source,
+    w_down,
+    w_bilinear,
+    w_up,
+    w_residual,
+    w_atom,
+):
+    cap = triplet_in.shape[0] // n
+    if cap % WIN or cap & (cap - 1) or n & (n - 1):
+        return plain_on_device(
+            edge_state,
+            atom_state,
+            atom_sends,
+            edge_source,
+            edge_target,
+            send_edges,
+            triplet_in,
+            triplet_out,
+            triplet_valid,
+            triplet_basis,
+            return_edges,
+            w_edge,
+            w_source,
+            w_down,
+            w_bilinear,
+            w_up,
+            w_residual,
+            w_atom,
+        )
+    edge_count, edge_width = edge_state.shape
+    atom_count, atom_width = atom_state.shape
+    basis_count = triplet_basis.shape[0]
+    width = w_down.shape[1]
+    slots = atom_sends.shape[0] // n
+    bf16 = jnp.bfloat16
+    loaded = (
+        atom_state,
+        atom_sends.reshape(1, -1),
+        edge_state,
+        w_edge,
+        edge_source.reshape(1, -1),
+        w_source,
+        w_down.T,
+        w_bilinear,
+        w_residual,
+        send_edges.reshape(n, 1, cap),
+        return_edges.reshape(n, 1, cap),
+        edge_target.reshape(1, -1),
+        w_up,
+        w_atom,
+    )
+    group = 2 if n % 2 == 0 else 1
+    return pl.pallas_call(
+        functools.partial(block_kernel, n, len(loaded)),
+        out_shape=(
+            jax.ShapeDtypeStruct((edge_count, edge_width), bf16),
+            jax.ShapeDtypeStruct((atom_count, atom_width), bf16),
+        ),
+        in_specs=[pl.BlockSpec(memory_space=pl.ANY)] * (len(loaded) + 4),
+        out_specs=(pl.BlockSpec(memory_space=pltpu.VMEM),) * 2,
+        scratch_shapes=[pltpu.VMEM(each.shape, each.dtype) for each in loaded]
+        + [
+            pltpu.VMEM((n, 1, cap), jnp.int32),
+            pltpu.VMEM((n, 1, cap), jnp.int32),
+            pltpu.VMEM((n, 1, cap), jnp.int32),
+            pltpu.VMEM((n, basis_count, cap), bf16),
+            pltpu.VMEM((n, slots, atom_width), bf16),
+            pltpu.VMEM((n, slots, atom_width), bf16),
+            pltpu.VMEM((edge_count, edge_width), jnp.float32),
+            pltpu.VMEM((basis_count * width, edge_count), bf16),
+            pltpu.VMEM((group, basis_count * width, cap), jnp.float32),
+            pltpu.VMEM((width, edge_count), jnp.float32),
+            pltpu.SemaphoreType.DMA((len(loaded),)),
+            pltpu.SemaphoreType.DMA((5, n)),
+            pltpu.SemaphoreType.DMA((5, n)),
+        ],
+        compiler_params=pltpu.CompilerParams(collective_id=0, has_side_effects=True),
+        name="block",
+    )(
+        *loaded,
+        triplet_in.reshape(n, 1, cap),
+        triplet_out.reshape(n, 1, cap),
+        triplet_valid.reshape(n, 1, cap),
+        triplet_basis,
+    )
+
+
 def solution(mesh):
     placed = (
         P(("groups", "graph"), None),
@@ -140,7 +451,7 @@
         P(),
     )
     return jax.shard_map(
-        on_device,
+        functools.partial(on_device, mesh.shape["graph"]),
         mesh=mesh,
         in_specs=placed,
         out_specs=(P(("groups", "graph"), None), P(("groups", "graph"), None)),

time: 141 us -> 28.2 us (0.20); the launches traced: 139 us -> 27.9 us
  matrix products: 61.6 us -> 0 us
  waiting for transfers between devices: 47.2 us -> 0 us
  Pallas kernels: 0 us -> 24.3 us
  starting transfers between devices: 18.9 us -> 0 us
  other arithmetic: 4.89 us -> 0 us
  local copies, waits for them, and re-layouts: 4.5 us -> 2.96 us
    dot_general x40 -> x0, matrix products: 61.6 us -> none  [the longest x24 39.5 us: matmul(): return jnp.dot(left, right, preferred_element_type=jnp.float32)]
    all_to_all x3 -> x0, waiting for transfers between devices: 47.2 us -> none  [the longest x1 22.6 us: on_device(): lax.all_to_all(pick_rows(send_edges, projected), 'graph', split_axis=0, c...]
    pallas_call x0 -> x1, Pallas kernels: none -> 24.3 us  [on_device(): pl.pallas_call(functools.partial(block_kernel, n, len(loaded)), out_shape...]
    all_to_all x3 -> x0, starting transfers between devices: 18.9 us -> none  [the longest x1 7.52 us: on_device(): lax.all_to_all(pick_rows(atom_sends, atom_state), 'graph', split_axis=0,...]
    while x32 -> x0, other arithmetic: 4.49 us -> none
    dot_general x16 -> x0, local copies, waits for them, and re-layouts: 1.95 us -> none  [bilinear_terms(): mixed = jnp.einsum('tkd,kt->td', expanded, coeffs.astype(jnp.float32))]
    unnamed x36 -> x2, local copies, waits for them, and re-layouts: 1.15 us -> 2.96 us
  transfers between devices with their start and end apart: 3 -> 0, of which waited for: 3 -> 0; matrix products, arithmetic and copies ran while one was open for 4% -> 0% of each run, Pallas kernels for 0% -> 0%
where the time goes in v2:
time: 28.2 us; the launch traced here: 27.9 us
  Pallas kernels  24.3 us (86%)
  local copies, waits for them, and re-layouts  2.96 us (10%)
  between operations  0.65 us (2%)
    pallas_call x1, Pallas kernels, on_device(): pl.pallas_call(functools.partial(block_kernel, n, len(loaded)), out_shape...  24.3 us
    unnamed x2, local copies, waits for them, and re-layouts  2.96 us

profile of v2, /device:TPU:0, one launch (start us, length us, event | category | flops | bytes accessed | tf_op | source)
XLA Modules:
  0.0 27.9 jit_solution(14003511730190383464)
XLA Ops:
  0.6 24.3 %block.1 = (bf16[256,512]{1,0:T(8,128)(2,1)}, bf16[16,256]{1,0:T(8,128)(2,1)}) custom-call(bf16[16,256]{1,0:T(8,128)(2,1)} %refs_0_.1, s32[1,128]{1,0:T(1,128)} %bitcast.17, bf16[256,512]{1,0:T(8,128)(2,1)} %refs_2_.1, bf16[512,512]{1,0:T(8,128)(2,1)} %refs_3_.1, s32[1,256]{1,0:T(1,128)} %bitcast.15, bf16[256,512]{1,0:T(8,128)(2,1)} %refs_5_.1, ...), custom_call_target="tpu_custom_call" | custom-call | tf_op jit(solution)/shard_map/block/pallas_call | solution.py:397
  25.0 1.7 %copy.22 = bf16[256,512]{1,0:T(8,128)(2,1)} copy(bf16[256,512]{1,0:T(8,128)(2,1)} %get-tuple-element.4) | data formatting | bytes 524288
  26.6 1.3 %copy.23 = bf16[16,256]{1,0:T(8,128)(2,1)} copy(bf16[16,256]{1,0:T(8,128)(2,1)} %get-tuple-element.5) | data formatting | bytes 16384

commit v3 on v2

--- a/solution.py
+++ b/solution.py
@@ -173,23 +173,34 @@
     return jnp.where(rows == spread, 1.0, 0.0).astype(jnp.bfloat16)
 
 
+def tail_kernel(sum_v, chain_v, atom_v, target_v, w_up_v, w_atom_v, edge_out_ref, atom_out_ref):
+    aggregate = sum_v[...].T.astype(jnp.bfloat16)
+    update = silu(matmul(aggregate, w_up_v[...]))
+    edge_out = (chain_v[...] + update).astype(jnp.bfloat16)
+    edge_out_ref[...] = edge_out
+    contrib = matmul(edge_out, w_atom_v[...]).astype(jnp.bfloat16)
+    atom_sum = matmul(hot_columns(atom_v.shape[0], target_v[...]), contrib)
+    atom_out_ref[...] = (atom_v[...].astype(jnp.float32) + silu(0.25 * atom_sum)).astype(
+        jnp.bfloat16
+    )
+
+
 def block_kernel(n, loaded, *refs):
     sources = refs[:loaded]
     in_hbm, out_hbm, valid_hbm, basis_hbm = refs[loaded : loaded + 4]
-    edge_out_ref, atom_out_ref = refs[loaded + 4 : loaded + 6]
+    chain_v, sum_v = refs[loaded + 4 : loaded + 6]
     held = refs[loaded + 6 : 2 * loaded + 6]
     (
-        in_v,
-        out_v,
-        valid_v,
+        stage_v,
+        ends_v,
+        stage_basis_v,
         basis_v,
         atoms_out,
         atoms_in,
-        chain_v,
         table_v,
         expand_v,
-        sum_v,
         load_sem,
+        stage_sem,
         send_sem,
         recv_sem,
     ) = refs[2 * loaded + 6 :]
@@ -205,12 +216,9 @@
         w_res_v,
         send_v,
         return_v,
-        target_v,
-        w_up_v,
-        w_atom_v,
     ) = held
     me = lax.axis_index("graph")
-    cap = in_v.shape[2]
+    cap = ends_v.shape[3]
     edge_count = edge_v.shape[0]
     width = w_down_v.shape[0]
     basis_count = basis_v.shape[1]
@@ -229,6 +237,13 @@
     ]
     for load in loads:
         load.start()
+    stages = [
+        pltpu.make_async_copy(src, stage_v.at[:, i], stage_sem.at[i])
+        for i, src in enumerate((in_hbm, out_hbm, valid_hbm))
+    ]
+    stages.append(pltpu.make_async_copy(basis_hbm, stage_basis_v, stage_sem.at[3]))
+    for stage in stages:
+        stage.start()
     loads[0].wait()
     loads[1].wait()
     picked = dot_at(hot_columns(atom_v.shape[0], asend_v[...]), atom_v[...], 0, 0)
@@ -239,14 +254,15 @@
         lanes = pl.ds(pl.multiple_of(peer * cap, cap), cap)
         return (
             (atoms_out.at[peer], atoms_in.at[me]),
-            (in_hbm.at[peer], in_v.at[me]),
-            (out_hbm.at[peer], out_v.at[me]),
-            (valid_hbm.at[peer], valid_v.at[me]),
-            (basis_hbm.at[:, lanes], basis_v.at[me]),
+            (stage_v.at[peer], ends_v.at[me]),
+            (stage_basis_v.at[:, lanes], basis_v.at[me]),
         )
 
     sent = []
-    for kinds in ((0,), (1, 2, 3, 4)):
+    for kinds in ((0,), (1, 2)):
+        if kinds[0]:
+            for stage in stages:
+                stage.wait()
         for step in range(n):
             peer = partner(me, step, n)
             for kind in kinds:
@@ -299,31 +315,20 @@
             step = group * expand_v.shape[0] + slot
             tile = partner(me, step, n)
             tiles.append(tile)
-            arrive(1, in_v, step, tile)
-            arrive(2, out_v, step, tile)
-            arrive(3, valid_v, step, tile)
-            arrive(4, basis_v, step, tile)
+            arrive(1, ends_v, step, tile)
+            arrive(2, basis_v, step, tile)
         for slot, tile in enumerate(tiles):
-            in_hot = hot_from(edge_count, look_up(send_v[tile], in_v[tile] & (cap - 1)))
+            in_hot = hot_from(edge_count, look_up(send_v[tile], ends_v[tile, 0] & (cap - 1)))
             expand_v[slot] = matmul(table_v[...], in_hot)
-            coeffs = basis_v[tile].astype(jnp.float32) * valid_v[tile].astype(jnp.float32)
+            coeffs = basis_v[tile].astype(jnp.float32) * ends_v[tile, 2].astype(jnp.float32)
             mixed = jnp.zeros((width, cap), jnp.float32)
             for k in range(basis_count):
                 mixed = mixed + coeffs[k : k + 1, :] * expand_v[slot, k * width : (k + 1) * width, :]
-            out_hot = hot_from(edge_count, look_up(return_v[tile], out_v[tile] & (cap - 1)))
+            out_hot = hot_from(edge_count, look_up(return_v[tile], ends_v[tile, 1] & (cap - 1)))
             sum_v[...] += dot_at(mixed.astype(jnp.bfloat16), out_hot, 1, 1)
         return carry
 
     lax.fori_loop(0, n // expand_v.shape[0], some_tiles, 0)
-    aggregate = sum_v[...].T.astype(jnp.bfloat16)
-    update = silu(matmul(aggregate, w_up_v[...]))
-    edge_out = (chain_v[...] + update).astype(jnp.bfloat16)
-    edge_out_ref[...] = edge_out
-    contrib = matmul(edge_out, w_atom_v[...]).astype(jnp.bfloat16)
-    atom_sum = matmul(hot_columns(atom_v.shape[0], target_v[...]), contrib)
-    atom_out_ref[...] = (atom_v[...].astype(jnp.float32) + silu(0.25 * atom_sum)).astype(
-        jnp.bfloat16
-    )
     for copy in sent:
         copy.wait_send()
 
@@ -389,34 +394,30 @@
         w_residual,
         send_edges.reshape(n, 1, cap),
         return_edges.reshape(n, 1, cap),
-        edge_target.reshape(1, -1),
-        w_up,
-        w_atom,
-    )
-    group = 2 if n % 2 == 0 else 1
-    return pl.pallas_call(
+    )
+    group = 4 if n % 4 == 0 else 1
+    chain, total = pl.pallas_call(
         functools.partial(block_kernel, n, len(loaded)),
         out_shape=(
-            jax.ShapeDtypeStruct((edge_count, edge_width), bf16),
-            jax.ShapeDtypeStruct((atom_count, atom_width), bf16),
+            jax.ShapeDtypeStruct((edge_count, edge_width), jnp.float32),
+            jax.ShapeDtypeStruct((width, edge_count), jnp.float32),
         ),
         in_specs=[pl.BlockSpec(memory_space=pl.ANY)] * (len(loaded) + 4),
         out_specs=(pl.BlockSpec(memory_space=pltpu.VMEM),) * 2,
         scratch_shapes=[pltpu.VMEM(each.shape, each.dtype) for each in loaded]
         + [
-            pltpu.VMEM((n, 1, cap), jnp.int32),
-            pltpu.VMEM((n, 1, cap), jnp.int32),
-            pltpu.VMEM((n, 1, cap), jnp.int32),
+            pltpu.VMEM((n, 3, 1, cap), jnp.int32),
+            pltpu.VMEM((n, 3, 1, cap), jnp.int32),
+            pltpu.VMEM(triplet_basis.shape, bf16),
             pltpu.VMEM((n, basis_count, cap), bf16),
             pltpu.VMEM((n, slots, atom_width), bf16),
             pltpu.VMEM((n, slots, atom_width), bf16),
-            pltpu.VMEM((edge_count, edge_width), jnp.float32),
             pltpu.VMEM((basis_count * width, edge_count), bf16),
             pltpu.VMEM((group, basis_count * width, cap), jnp.float32),
-            pltpu.VMEM((width, edge_count), jnp.float32),
             pltpu.SemaphoreType.DMA((len(loaded),)),
-            pltpu.SemaphoreType.DMA((5, n)),
-            pltpu.SemaphoreType.DMA((5, n)),
+            pltpu.SemaphoreType.DMA((4,)),
+            pltpu.SemaphoreType.DMA((3, n)),
+            pltpu.SemaphoreType.DMA((3, n)),
         ],
         compiler_params=pltpu.CompilerParams(collective_id=0, has_side_effects=True),
         name="block",
@@ -427,6 +428,16 @@
         triplet_valid.reshape(n, 1, cap),
         triplet_basis,
     )
+    return pl.pallas_call(
+        tail_kernel,
+        out_shape=(
+            jax.ShapeDtypeStruct((edge_count, edge_width), bf16),
+            jax.ShapeDtypeStruct((atom_count, atom_width), bf16),
+        ),
+        in_specs=[pl.BlockSpec(memory_space=pltpu.VMEM)] * 6,
+        out_specs=(pl.BlockSpec(memory_space=pltpu.VMEM),) * 2,
+        name="tail",
+    )(total, chain, atom_state, edge_target.reshape(1, -1), w_up, w_atom)
 
 
 def solution(mesh):

time: 28.2 us -> 24.4 us (0.87)
  local copies, waits for them, and re-layouts: 2.96 us -> 0 us
  Pallas kernels: 24.3 us -> 23.5 us
    pallas_call x1, Pallas kernels: 24.3 us -> 21.1 us  [on_device(): pl.pallas_call(functools.partial(block_kernel, n, len(loaded)), out_shape...]
    unnamed x2 -> x0, local copies, waits for them, and re-layouts: 2.96 us -> none
    pallas_call x0 -> x1, Pallas kernels: none -> 2.39 us  [on_device(): pl.pallas_call(tail_kernel, out_shape=(jax.ShapeDtypeStruct((edge_count,...]
where the time goes in v3:
time: 24.4 us; the launch traced here: 24.1 us
  Pallas kernels  23.5 us (96%)
  between operations  0.64 us (3%)
    pallas_call x1, Pallas kernels, on_device(): pl.pallas_call(functools.partial(block_kernel, n, len(loaded)), out_shape...  21.1 us
    pallas_call x1, Pallas kernels, on_device(): pl.pallas_call(tail_kernel, out_shape=(jax.ShapeDtypeStruct((edge_count,...  2.39 us

profile of v3, /device:TPU:0, one launch (start us, length us, event | category | flops | bytes accessed | tf_op | source)
XLA Modules:
  0.0 24.1 jit_solution(5839060912040603054)
XLA Ops:
  0.6 21.1 %block.1 = (f32[256,512]{1,0:T(8,128)}, f32[64,256]{1,0:T(8,128)}) custom-call(bf16[16,256]{1,0:T(8,128)(2,1)} %atom_v.1, s32[1,128]{1,0:T(1,128)} %bitcast.17, bf16[256,512]{1,0:T(8,128)(2,1)} %refs_2_.1, bf16[512,512]{1,0:T(8,128)(2,1)} %refs_3_.1, s32[1,256]{1,0:T(1,128)} %bitcast.15, bf16[256,512]{1,0:T(8,128)(2,1)} %refs_5_.1, bf16[64,512]{1,0:T(8,128)(2,1)} %bitcast.9, ...), custom_call_target="tpu_custom_call" | custom-call | tf_op jit(solution)/shard_map/block/pallas_call | solution.py:399
  21.8 2.4 %tail.1 = (bf16[256,512]{1,0:T(8,128)(2,1)}, bf16[16,256]{1,0:T(8,128)(2,1)}) custom-call(f32[64,256]{1,0:T(8,128)} %get-tuple-element.4.sum_v, f32[256,512]{1,0:T(8,128)} %get-tuple-element.5.chain_v, bf16[16,256]{1,0:T(8,128)(2,1)} %atom_v.1, s32[1,256]{1,0:T(1,128)} %bitcast.16, bf16[64,512]{1,0:T(8,128)(2,1)} %w_up_v.1, bf16[512,256]{1,0:T(8,128)(2,1)} %w_atom_v.1), custom_call_target="tpu_custom_call" | custom-call | tf_op jit(solution)/shard_map/tail/pallas_call | solution.py:431
